TPU v7x, 256 devices: a whole 4x4x8 slice. The times are simulated.
256 devices in a mesh: leaf: 256 (over z, y, x, core).
Axes of the slice: x: 4, y: 4, z: 8, core: 2. Of those that a mesh axis runs over, the one named last changes fastest.
Arguments:
- panels: bfloat16 [512, 64, 256], P('leaf'), may hold values from -6 to 6
- basis: bfloat16 [512, 64, 256], P('leaf'), may hold values from -0.375 to 0.375
- transfer: bfloat16 [512, 64, 64], P('leaf'), may hold values from -0.25 to 0.25
- near_blocks: bfloat16 [512, 27, 256, 256], P('leaf'), may hold values from -0.078125 to 0.078125
- coupling: bfloat16 [2, 343, 4096], replicated, may hold values from -0.0546875 to 0.0546875
- near_list: int32 [512, 27], P('leaf'), may hold values from -1 to 511, as said below
Outputs:
- product: bfloat16 [512, 64, 256], P('leaf')
Inputs may be any that keep to these rules, and one draw needn't show every extreme that they name: `near_list`: row i lists, in an order of no meaning, leaf i and the leaves whose grid positions differ from it by at most one in each coordinate; -1 fills the other slots.
All inputs are finite; a program needn't handle non-finite values.
Results may differ from a plain program's by a relative error of at most 0.0035.
Values may be sent and summed in bfloat16 or wider, within the bound.
A program may use at most 192 MiB of HBM per device.

v0:
```python
import jax
import jax.numpy as jnp
from jax import lax
from jax.experimental import pallas as pl
from jax.experimental.pallas import tpu as pltpu
from jax.sharding import PartitionSpec as P

MESH = pl.DeviceIdType.MESH
AXIS = "leaf"
LEAF = 256
RANK = 64
COLS = 64
NNEAR = 27
SHIFTS = 343
HALF = RANK // 2
PAIR = 2 * COLS
ZERO_SLOT = 36
GROUP = 7


def bit(value, k):
    return (value // (1 << k)) % 2


def device_position(dev):
    bx = bit(dev, 2) + 2 * bit(dev, 5)
    y = bit(dev, 0) + 2 * bit(dev, 3) + 4 * bit(dev, 6)
    z = bit(dev, 1) + 2 * bit(dev, 4) + 4 * bit(dev, 7)
    return bx, y, z


def device_at(bx, y, z):
    return (
        y % 2
        + 2 * (z % 2)
        + 4 * (bx % 2)
        + 8 * ((y // 2) % 2)
        + 16 * ((z // 2) % 2)
        + 32 * (bx // 2)
        + 64 * (y // 4)
        + 128 * (z // 4)
    )


def cluster_position(p):
    px = bit(p, 0) + 2 * bit(p, 3)
    py = bit(p, 1) + 2 * bit(p, 4)
    pz = bit(p, 2) + 2 * bit(p, 5)
    return px, py, pz


def cluster_at(px, py, pz):
    return (
        px % 2
        + 2 * (py % 2)
        + 4 * (pz % 2)
        + 8 * (px // 2)
        + 16 * (py // 2)
        + 32 * (pz // 2)
    )


def within(value, size):
    return (value >= 0) & (value < size)


def split_rows(scratch, value):
    scratch[...] = value
    even = scratch[pl.ds(0, HALF, stride=2), :]
    odd = scratch[pl.ds(1, HALF, stride=2), :]
    return jnp.concatenate([even, odd], axis=1)


def split_levels(raw, turn, tables):
    group = turn.shape[0] // RANK

    def split(i, carry):
        first = i * group
        turn[...] = raw[pl.ds(first, group)].reshape(group * RANK, PAIR).astype(jnp.float32)
        for level, table in enumerate(tables):
            rows = turn[pl.ds(level, group * HALF, stride=2), :]
            table[pl.ds(first, group)] = rows.astype(jnp.bfloat16).reshape(group, HALF, PAIR)
        return carry

    lax.fori_loop(0, SHIFTS // group, split, 0)


def kernel(
    panels_ref,
    basis_ref,
    transfer_ref,
    near_ref,
    coupling_ref,
    list_ref,
    out_ref,
    pbuf,
    nbuf,
    basis_vmem,
    transfer_vmem,
    raw,
    m0,
    m1,
    x0,
    x1,
    x1_own,
    cluster_send,
    cluster_recv,
    sum_send,
    sum_recv,
    tmp,
    turn,
    xt,
    load_sem,
    panel_send_sem,
    panel_recv_sem,
    coef_send_sem,
    coef_recv_sem,
    part_send_sem,
    part_recv_sem,
    clus_send_sem,
    clus_recv_sem,
    sum_send_sem,
    sum_recv_sem,
):
    me = lax.axis_index(AXIS)
    g = me % 4
    gy = me % 2
    gz = (me // 2) % 2
    parent = me // 4
    bx, y, z = device_position(me)
    px, py, pz = cluster_position(parent)
    own_slot = 17

    load_panels = pltpu.make_async_copy(panels_ref, pbuf.at[pl.ds(own_slot, 2)], load_sem.at[0])
    load_panels.start()
    load_basis = pltpu.make_async_copy(basis_ref, basis_vmem, load_sem.at[1])
    load_basis.start()
    load_transfer = pltpu.make_async_copy(transfer_ref, transfer_vmem, load_sem.at[2])
    load_transfer.start()
    load_raw = pltpu.make_async_copy(coupling_ref, raw, load_sem.at[3])
    load_raw.start()
    load_near = pltpu.make_async_copy(near_ref, nbuf, load_sem.at[4])
    load_near.start()

    x0[...] = jnp.zeros_like(x0)
    x1[...] = jnp.zeros_like(x1)
    pbuf[ZERO_SLOT] = jnp.zeros((COLS, LEAF), jnp.bfloat16)

    def panel_partner(i):
        ox, oy, oz = i // 9 - 1, (i // 3) % 3 - 1, i % 3 - 1
        tx, ty, tz = bx + ox, y + oy, z + oz
        there = within(tx, 4) & within(ty, 8) & within(tz, 8) & (i != 13)
        return device_at(tx, ty, tz), there, ox, oy, oz

    def coef_partner(i):
        tx, ty, tz = px + i // 9 - 1, py + (i // 3) % 3 - 1, pz + i % 3 - 1
        there = within(tx, 4) & within(ty, 4) & within(tz, 4) & (i != 13)
        return 4 * cluster_at(tx, ty, tz) + g, there

    def cluster_far(other):
        qx, qy, qz = cluster_position(other)
        dx, dy, dz = qx - px, qy - py, qz - pz
        near = within(dx + 1, 3) & within(dy + 1, 3) & within(dz + 1, 3)
        return jnp.logical_not(near)

    barrier = pltpu.get_barrier_semaphore()

    def greet(dev, there):
        @pl.when(there)
        def _():
            pl.semaphore_signal(barrier, inc=1, device_id=(dev,), device_id_type=MESH)

        return jnp.where(there, 1, 0)

    def greet_near(i, count):
        dev, there, _, _, _ = panel_partner(i)
        count = count + greet(dev, there)
        dev, there = coef_partner(i)
        return count + greet(dev, there)

    def greet_cluster(i, count):
        return count + greet(4 * (4 * i + g) + parent % 4, cluster_far(4 * i + g))

    count = lax.fori_loop(0, 27, greet_near, 0)
    count = lax.fori_loop(0, 16, greet_cluster, count)
    for r in range(1, 4):
        pl.semaphore_signal(
            barrier, inc=1, device_id=(4 * parent + (g + r) % 4,), device_id_type=MESH
        )
    count = count + 3

    load_panels.wait()
    load_basis.wait()
    load_transfer.wait()
    part = jnp.zeros((RANK, COLS), jnp.float32)
    for h in range(2):
        coef = lax.dot_general(
            basis_vmem[h],
            pbuf[own_slot + h],
            (((1,), (1,)), ((), ())),
            preferred_element_type=jnp.float32,
        )
        x0[13, pl.ds(HALF * h, HALF), :] = split_rows(tmp, coef).astype(jnp.bfloat16)
        part = part + lax.dot_general(
            transfer_vmem[h],
            coef.astype(jnp.bfloat16),
            (((0,), (0,)), ((), ())),
            preferred_element_type=jnp.float32,
        )
    cluster_send[...] = split_rows(tmp, part)

    pl.semaphore_wait(barrier, count)

    def part_copy(r):
        return pltpu.make_async_remote_copy(
            src_ref=cluster_send,
            dst_ref=cluster_recv.at[r - 1],
            send_sem=part_send_sem.at[r - 1],
            recv_sem=part_recv_sem.at[r - 1],
            device_id=(4 * parent + (g + r) % 4,),
            device_id_type=MESH,
        )

    for r in range(1, 4):
        part_copy(r).start()

    def coef_copy(i, slot, dev):
        return pltpu.make_async_remote_copy(
            src_ref=x0.at[13],
            dst_ref=x0.at[slot],
            send_sem=coef_send_sem.at[i],
            recv_sem=coef_recv_sem.at[slot],
            device_id=(dev,),
            device_id_type=MESH,
        )

    def send_coef(i, carry):
        dev, there = coef_partner(i)

        @pl.when(there)
        def _():
            coef_copy(i, 26 - i, dev).start()

        return carry

    lax.fori_loop(0, 27, send_coef, 0)

    def panel_copy(i, dev, leaf, leaves, slot):
        return pltpu.make_async_remote_copy(
            src_ref=pbuf.at[pl.ds(own_slot + leaf, leaves)],
            dst_ref=pbuf.at[pl.ds(slot, leaves)],
            send_sem=panel_send_sem.at[i],
            recv_sem=panel_recv_sem.at[26 - i],
            device_id=(dev,),
            device_id_type=MESH,
        )

    x_steps = ((0, 1, 3), (0, 2, 1), (1, 1, 0))

    def send_panel(j, carry):
        for step, (leaf, leaves, place) in enumerate(x_steps):
            i = 9 * step + j
            dev, there, _, oy, oz = panel_partner(i)

            @pl.when(there)
            def _():
                slot = ((1 - oz) * 3 + 1 - oy) * 4 + place
                panel_copy(i, dev, leaf, leaves, slot).start()

        return carry

    for r in range(1, 4):
        part_copy(r).wait_recv()
    total = cluster_send[...] + cluster_recv[0] + cluster_recv[1] + cluster_recv[2]
    x1_own[...] = total.astype(jnp.bfloat16)

    def clus_copy(i, slot, dev):
        return pltpu.make_async_remote_copy(
            src_ref=x1_own,
            dst_ref=x1.at[slot],
            send_sem=clus_send_sem.at[i],
            recv_sem=clus_recv_sem.at[slot],
            device_id=(dev,),
            device_id_type=MESH,
        )

    def send_cluster(i, carry):
        @pl.when(cluster_far(4 * i + g))
        def _():
            clus_copy(i, parent // 4, 4 * (4 * i + g) + parent % 4).start()

        return carry

    lax.fori_loop(0, 16, send_cluster, 0)
    lax.fori_loop(0, 9, send_panel, 0)

    load_raw.wait()
    split_levels(raw, turn, (m0, m1))
    for table in (m0, m1):
        for dx in (2, 3, 4):
            for dy in (2, 3, 4):
                first = 49 * dx + 7 * dy + 2
                table[pl.ds(first, 3)] = jnp.zeros((3, HALF, PAIR), jnp.bfloat16)

    def wait_coef(i, carry):
        _, there = coef_partner(i)

        @pl.when(there)
        def _():
            coef_copy(i, i, me).wait_recv()

        return carry

    lax.fori_loop(0, 27, wait_coef, 0)
    offsets = [(a, b, c) for a in (-1, 0, 1) for b in (-1, 0, 1) for c in (-1, 0, 1)]
    chunks = [list(range(first, min(first + 4, 27))) for first in range(0, 27, 4)]
    for t, chunk in enumerate(chunks):
        rows = x0[pl.ds(chunk[0], len(chunk))].reshape(len(chunk) * RANK, PAIR)
        xt[t, :, : len(chunk) * RANK] = rows.T
    lanes = lax.broadcasted_iota(jnp.int32, (COLS, PAIR), 1)
    base = 7 * gy + gz
    for tz in range(2):
        for ty in range(2):
            acc = jnp.zeros((PAIR, 2 * PAIR), jnp.float32)
            for t, chunk in enumerate(chunks):
                columns = []
                for tx in range(2):
                    column = []
                    for e in chunk:
                        ex, ey, ez = offsets[e]
                        for h in range(2):
                            code = (
                                49 * (2 * ex + h - tx + 3)
                                + 7 * (2 * ey - ty + 3)
                                + (2 * ez - tz + 3)
                            )
                            column.append(m0[base + code])
                    columns.append(jnp.concatenate(column, axis=0))
                weights = jnp.concatenate(columns, axis=1)
                acc = acc + jnp.dot(
                    xt[t, :, : len(chunk) * RANK], weights, preferred_element_type=jnp.float32
                )
            first = acc[:COLS, :PAIR] + pltpu.roll(acc[COLS:, :PAIR], COLS, 1)
            second = pltpu.roll(acc[:COLS, PAIR:], COLS, 1) + acc[COLS:, PAIR:]
            sum_send[2 * tz + ty, :COLS, :] = jnp.where(lanes < COLS, first, second)

    def wait_cluster(i, carry):
        @pl.when(cluster_far(4 * i + g))
        def _():
            clus_copy(i, i, me).wait_recv()

        return carry

    lax.fori_loop(0, 16, wait_cluster, 0)
    acc = jnp.zeros((PAIR, PAIR), jnp.float32)
    for t in range(2):
        column = []
        for i in range(8 * t, 8 * t + 8):
            qx, qy, qz = cluster_position(4 * i + g)
            column.append(m1[49 * (qx - px + 3) + 7 * (qy - py + 3) + (qz - pz + 3)])
        rows = x1[pl.ds(8 * t, 8)].reshape(8 * HALF, PAIR)
        acc = acc + jnp.dot(
            rows.T, jnp.concatenate(column, axis=0), preferred_element_type=jnp.float32
        )
    down = acc[:COLS] + pltpu.roll(acc[COLS:], COLS, 1)
    down = jnp.where(lanes[:HALF] < COLS, down[:HALF], pltpu.roll(down[HALF:], COLS, 1))
    for n in range(4):
        sum_send[n, COLS:, :] = down

    def sum_copy(r):
        return pltpu.make_async_remote_copy(
            src_ref=sum_send.at[(g + r) % 4],
            dst_ref=sum_recv.at[r - 1],
            send_sem=sum_send_sem.at[r - 1],
            recv_sem=sum_recv_sem.at[r - 1],
            device_id=(4 * parent + (g + r) % 4,),
            device_id_type=MESH,
        )

    for r in range(1, 4):
        sum_copy(r).start()

    def wait_panel(j, carry):
        for step, (leaf, leaves, place) in enumerate(x_steps):
            i = 9 * step + j
            _, there, _, oy, oz = panel_partner(i)

            @pl.when(there)
            def _():
                slot = ((1 - oz) * 3 + 1 - oy) * 4 + place
                panel_copy(26 - i, me, 0, leaves, slot).wait_recv()

        return carry

    lax.fori_loop(0, 9, wait_panel, 0)
    load_near.wait()

    def slot_of(entry):
        lx = ((entry >> 0) & 1) + 2 * ((entry >> 3) & 1) + 4 * ((entry >> 6) & 1)
        ly = ((entry >> 1) & 1) + 2 * ((entry >> 4) & 1) + 4 * ((entry >> 7) & 1)
        lz = ((entry >> 2) & 1) + 2 * ((entry >> 5) & 1) + 4 * ((entry >> 8) & 1)
        slot = ((lz - z + 1) * 3 + ly - y + 1) * 4 + lx - 2 * bx + 1
        return jnp.where(entry < 0, ZERO_SLOT, jnp.clip(slot, 0, ZERO_SLOT))

    near_terms = []
    for h in range(2):
        acc = jnp.zeros((COLS, LEAF), jnp.float32)
        for k in range(NNEAR):
            acc = acc + jnp.dot(
                pbuf[slot_of(list_ref[h, k])], nbuf[h, k], preferred_element_type=jnp.float32
            )
        near_terms.append(acc)

    for r in range(1, 4):
        sum_copy(r).wait_recv()
    sums = sum_send[g] + sum_recv[0] + sum_recv[1] + sum_recv[2]
    down = jnp.concatenate([sums[COLS:, :COLS], sums[COLS:, COLS:]], axis=0).astype(jnp.bfloat16)
    for h in range(2):
        far_coef = sums[:COLS, COLS * h : COLS * (h + 1)] + lax.dot_general(
            down,
            transfer_vmem[h],
            (((1,), (1,)), ((), ())),
            preferred_element_type=jnp.float32,
        )
        far_term = jnp.dot(
            far_coef.astype(jnp.bfloat16), basis_vmem[h], preferred_element_type=jnp.float32
        )
        out_ref[h] = (near_terms[h] + far_term).astype(jnp.bfloat16)

    for r in range(1, 4):
        part_copy(r).wait_send()
        sum_copy(r).wait_send()

    def drain(i, carry):
        dev, there = coef_partner(i)

        @pl.when(there)
        def _():
            coef_copy(i, 26 - i, dev).wait_send()

        return carry

    lax.fori_loop(0, 27, drain, 0)

    def drain_cluster(i, carry):
        @pl.when(cluster_far(4 * i + g))
        def _():
            clus_copy(i, parent // 4, 4 * (4 * i + g) + parent % 4).wait_send()

        return carry

    lax.fori_loop(0, 16, drain_cluster, 0)

    def drain_panel(j, carry):
        for step, (leaf, leaves, place) in enumerate(x_steps):
            i = 9 * step + j
            dev, there, _, oy, oz = panel_partner(i)

            @pl.when(there)
            def _():
                slot = ((1 - oz) * 3 + 1 - oy) * 4 + place
                panel_copy(i, dev, leaf, leaves, slot).wait_send()

        return carry

    lax.fori_loop(0, 9, drain_panel, 0)


def per_device(panels, basis, transfer, near_blocks, coupling, near_list):
    tables = coupling.reshape(2, SHIFTS, HALF, PAIR).transpose(1, 2, 0, 3)
    tables = tables.reshape(SHIFTS, RANK, PAIR)
    vmem = pl.BlockSpec(memory_space=pltpu.VMEM)
    hbm = pl.BlockSpec(memory_space=pltpu.HBM)
    dma = pltpu.SemaphoreType.DMA
    return pl.pallas_call(
        kernel,
        name="h2_product",
        out_shape=jax.ShapeDtypeStruct((2, COLS, LEAF), jnp.bfloat16),
        in_specs=[hbm, hbm, hbm, hbm, hbm, pl.BlockSpec(memory_space=pltpu.SMEM)],
        out_specs=vmem,
        scratch_shapes=[
            pltpu.VMEM((37, COLS, LEAF), jnp.bfloat16),
            pltpu.VMEM((2, NNEAR, LEAF, LEAF), jnp.bfloat16),
            pltpu.VMEM((2, RANK, LEAF), jnp.bfloat16),
            pltpu.VMEM((2, RANK, RANK), jnp.bfloat16),
            pltpu.VMEM((SHIFTS, RANK, PAIR), jnp.bfloat16),
            pltpu.VMEM((SHIFTS, HALF, PAIR), jnp.bfloat16),
            pltpu.VMEM((SHIFTS, HALF, PAIR), jnp.bfloat16),
            pltpu.VMEM((27, RANK, PAIR), jnp.bfloat16),
            pltpu.VMEM((16, HALF, PAIR), jnp.bfloat16),
            pltpu.VMEM((HALF, PAIR), jnp.bfloat16),
            pltpu.VMEM((HALF, PAIR), jnp.float32),
            pltpu.VMEM((3, HALF, PAIR), jnp.float32),
            pltpu.VMEM((4, COLS + HALF, PAIR), jnp.float32),
            pltpu.VMEM((3, COLS + HALF, PAIR), jnp.float32),
            pltpu.VMEM((RANK, COLS), jnp.float32),
            pltpu.VMEM((GROUP * RANK, PAIR), jnp.float32),
            pltpu.VMEM((7, PAIR, 2 * PAIR), jnp.bfloat16),
            dma((5,)),
            dma((27,)),
            dma((27,)),
            dma((27,)),
            dma((27,)),
            dma((3,)),
            dma((3,)),
            dma((16,)),
            dma((16,)),
            dma((3,)),
            dma((3,)),
        ],
        compiler_params=pltpu.CompilerParams(
            collective_id=0, has_side_effects=True, vmem_limit_bytes=56 << 20
        ),
    )(panels, basis, transfer, near_blocks, tables, near_list)


def solution(mesh):
    return jax.shard_map(
        per_device,
        mesh=mesh,
        in_specs=(
            P(AXIS, None, None),
            P(AXIS, None, None),
            P(AXIS, None, None),
            P(AXIS, None, None, None),
            P(),
            P(AXIS, None),
        ),
        out_specs=P(AXIS, None, None),
        check_vma=False,
    )
```

profile of v0, /device:TPU:62, one launch (start us, length us, event | category | flops | bytes accessed | tf_op | source)
XLA Modules:
  0.0 48.4 jit_solution(14841976122622303213)
XLA Ops:
  0.0 46.9 %h2_product.1 = bf16[2,64,256]{2,1,0:T(8,128)(2,1)} custom-call(bf16[2,64,256]{2,1,0:T(8,128)(2,1)} %panels_ref.1, bf16[2,64,256]{2,1,0:T(8,128)(2,1)} %basis_ref.1, bf16[2,64,64]{2,1,0:T(8,128)(2,1)} %transfer_ref.1, bf16[2,27,256,256]{3,2,1,0:T(8,128)(2,1)} %near_ref.1, bf16[343,64,128]{2,1,0:T(8,128)(2,1)} %bitcast.5, s32[2,27]{1,0:T(2,128)} %list_ref.1), custom_call_target="tpu_custom_call" | custom-call | tf_op jit(solution)/shard_map/h2_product/pallas_call | solution.py:475
  46.9 1.5 %copy.9 = bf16[2,64,256]{2,1,0:T(8,128)(2,1)} copy(bf16[2,64,256]{2,1,0:T(8,128)(2,1)} %h2_product.1) | data formatting | bytes 131072
where the time goes:
time: 48.5 us; the launch traced here: 48.4 us
  Pallas kernels  46.9 us (97%)
  local copies, waits for them, and re-layouts  1.47 us (3%)
    pallas_call x1, Pallas kernels, per_device(): pl.pallas_call(kernel, name='h2_product', out_shape=jax.ShapeDtypeStruct(...  46.9 us
    unnamed x1, local copies, waits for them, and re-layouts  1.47 us

commit v1 on v0

--- a/solution.py
+++ b/solution.py
@@ -29,19 +29,6 @@
     return bx, y, z
 
 
-def device_at(bx, y, z):
-    return (
-        y % 2
-        + 2 * (z % 2)
-        + 4 * (bx % 2)
-        + 8 * ((y // 2) % 2)
-        + 16 * ((z // 2) % 2)
-        + 32 * (bx // 2)
-        + 64 * (y // 4)
-        + 128 * (z // 4)
-    )
-
-
 def cluster_position(p):
     px = bit(p, 0) + 2 * bit(p, 3)
     py = bit(p, 1) + 2 * bit(p, 4)
@@ -49,19 +36,31 @@
     return px, py, pz
 
 
-def cluster_at(px, py, pz):
-    return (
-        px % 2
-        + 2 * (py % 2)
-        + 4 * (pz % 2)
-        + 8 * (px // 2)
-        + 16 * (py // 2)
-        + 32 * (pz // 2)
-    )
-
-
-def within(value, size):
-    return (value >= 0) & (value < size)
+OFFSETS = [(a, b, c) for a in (-1, 0, 1) for b in (-1, 0, 1) for c in (-1, 0, 1)]
+CENTRE = 13
+
+
+def neighbours(position, sizes, weights):
+    axes = []
+    for here, size, bits in zip(position, sizes, weights):
+        steps = {}
+        for step in (-1, 0, 1):
+            there = here + step
+            share = sum(weight * bit(there, k) for k, weight in enumerate(bits))
+            steps[step] = (share, {-1: here > 0, 0: None, 1: here < size - 1}[step])
+        axes.append(steps)
+    found = []
+    for offset in OFFSETS:
+        parts = [axes[a][offset[a]] for a in range(3)]
+        valid = [ok for _, ok in parts if ok is not None]
+        there = None
+        for ok in valid:
+            there = ok if there is None else there & ok
+        found.append((sum(share for share, _ in parts), there))
+    total = 1
+    for here, size in zip(position, sizes):
+        total = total * (1 + jnp.where(here > 0, 1, 0) + jnp.where(here < size - 1, 1, 0))
+    return found, total - 1
 
 
 def split_rows(scratch, value):
@@ -91,10 +90,11 @@
     transfer_ref,
     near_ref,
     coupling_ref,
-    list_ref,
+    list_hbm,
     out_ref,
     pbuf,
     nbuf,
+    list_ref,
     basis_vmem,
     transfer_vmem,
     raw,
@@ -137,6 +137,8 @@
     load_basis.start()
     load_transfer = pltpu.make_async_copy(transfer_ref, transfer_vmem, load_sem.at[2])
     load_transfer.start()
+    load_list = pltpu.make_async_copy(list_hbm, list_ref, load_sem.at[5])
+    load_list.start()
     load_raw = pltpu.make_async_copy(coupling_ref, raw, load_sem.at[3])
     load_raw.start()
     load_near = pltpu.make_async_copy(near_ref, nbuf, load_sem.at[4])
@@ -146,48 +148,62 @@
     x1[...] = jnp.zeros_like(x1)
     pbuf[ZERO_SLOT] = jnp.zeros((COLS, LEAF), jnp.bfloat16)
 
-    def panel_partner(i):
-        ox, oy, oz = i // 9 - 1, (i // 3) % 3 - 1, i % 3 - 1
-        tx, ty, tz = bx + ox, y + oy, z + oz
-        there = within(tx, 4) & within(ty, 8) & within(tz, 8) & (i != 13)
-        return device_at(tx, ty, tz), there, ox, oy, oz
-
-    def coef_partner(i):
-        tx, ty, tz = px + i // 9 - 1, py + (i // 3) % 3 - 1, pz + i % 3 - 1
-        there = within(tx, 4) & within(ty, 4) & within(tz, 4) & (i != 13)
-        return 4 * cluster_at(tx, ty, tz) + g, there
-
-    def cluster_far(other):
-        qx, qy, qz = cluster_position(other)
-        dx, dy, dz = qx - px, qy - py, qz - pz
-        near = within(dx + 1, 3) & within(dy + 1, 3) & within(dz + 1, 3)
-        return jnp.logical_not(near)
+    def ones(flags):
+        return sum(jnp.where(flag, 1, 0) for flag in flags)
+
+    def place_of(position):
+        tx, ty, tz = position
+        share_x = 4 * bit(tx, 0) + 32 * bit(tx, 1)
+        share_y = bit(ty, 0) + 8 * bit(ty, 1) + 64 * bit(ty, 2)
+        share_z = 2 * bit(tz, 0) + 16 * bit(tz, 1) + 128 * bit(tz, 2)
+        return share_x + share_y + share_z
+
+    side_x = [(place_of((bx + d, y, z)), ok) for d, ok in ((-1, bx > 0), (1, bx < 3))]
+    side_y = [(place_of((bx, y + d, z)), ok) for d, ok in ((-1, y > 0), (1, y < 7))]
+    side_z = [(place_of((bx, y, z + d)), ok) for d, ok in ((-1, z > 0), (1, z < 7))]
+    panel_count = ones([ok for _, ok in side_x + side_y + side_z])
+    coef_partners, coef_count = neighbours(
+        (px, py, pz), (4, 4, 4), ((4, 32), (8, 64), (16, 128))
+    )
+    coef_partners = [(dev + g, there) for dev, there in coef_partners]
+
+    def close(q, p):
+        return (q - p < 2) & (p - q < 2)
+
+    near_x = [close(gy + 2 * k, px) for k in range(2)]
+    near_y = [close(gz + 2 * k, py) for k in range(2)]
+    near_z = [close(k, pz) for k in range(4)]
+    clusters = []
+    for i in range(16):
+        kx, ky, kz = (i // 2) % 2, (i // 4) % 2, i % 2 + 2 * (i // 8)
+        near = near_x[kx] & near_y[ky] & near_z[kz]
+        dev = 16 * i + 4 * g + parent % 4
+        clusters.append((dev, jnp.logical_not(near), 98 * kx + 14 * ky + kz))
+    cluster_base = 49 * (gy - px + 3) + 7 * (gz - py + 3) + 3 - pz
+
+    cluster_count = 16 - ones(near_x) * ones(near_y) * ones(near_z)
+    mates = [4 * parent + (g + r) % 4 for r in range(1, 4)]
+
+    def for_each(partners, action):
+        for i, partner in enumerate(partners):
+            if partner[1] is None:
+                continue
+
+            @pl.when(partner[1])
+            def _():
+                action(i, partner[0])
 
     barrier = pltpu.get_barrier_semaphore()
 
-    def greet(dev, there):
-        @pl.when(there)
-        def _():
-            pl.semaphore_signal(barrier, inc=1, device_id=(dev,), device_id_type=MESH)
-
-        return jnp.where(there, 1, 0)
-
-    def greet_near(i, count):
-        dev, there, _, _, _ = panel_partner(i)
-        count = count + greet(dev, there)
-        dev, there = coef_partner(i)
-        return count + greet(dev, there)
-
-    def greet_cluster(i, count):
-        return count + greet(4 * (4 * i + g) + parent % 4, cluster_far(4 * i + g))
-
-    count = lax.fori_loop(0, 27, greet_near, 0)
-    count = lax.fori_loop(0, 16, greet_cluster, count)
-    for r in range(1, 4):
-        pl.semaphore_signal(
-            barrier, inc=1, device_id=(4 * parent + (g + r) % 4,), device_id_type=MESH
-        )
-    count = count + 3
+    def greet(i, dev):
+        pl.semaphore_signal(barrier, inc=1, device_id=(dev,), device_id_type=MESH)
+
+    for dev in mates:
+        greet(0, dev)
+    for_each(side_x + side_y + side_z, greet)
+    for_each(coef_partners, greet)
+    for_each(clusters, greet)
+    count = panel_count + coef_count + cluster_count + 3
 
     load_panels.wait()
     load_basis.wait()
@@ -217,7 +233,7 @@
             dst_ref=cluster_recv.at[r - 1],
             send_sem=part_send_sem.at[r - 1],
             recv_sem=part_recv_sem.at[r - 1],
-            device_id=(4 * parent + (g + r) % 4,),
+            device_id=(mates[r - 1],),
             device_id_type=MESH,
         )
 
@@ -234,40 +250,70 @@
             device_id_type=MESH,
         )
 
-    def send_coef(i, carry):
-        dev, there = coef_partner(i)
-
-        @pl.when(there)
-        def _():
-            coef_copy(i, 26 - i, dev).start()
-
-        return carry
-
-    lax.fori_loop(0, 27, send_coef, 0)
-
-    def panel_copy(i, dev, leaf, leaves, slot):
+    for_each(coef_partners, lambda i, dev: coef_copy(i, 26 - i, dev).start())
+
+    layer_ok = (side_z[0][1], None, side_z[1][1])
+    spans = ((1, 2, None), (0, 1, side_x[0][1]), (3, 1, side_x[1][1]))
+
+    def both(*flags):
+        result = None
+        for flag in flags:
+            if flag is not None:
+                result = flag if result is None else result & flag
+        return result
+
+    def panel_copy(source, target, leaves, index, dev):
         return pltpu.make_async_remote_copy(
-            src_ref=pbuf.at[pl.ds(own_slot + leaf, leaves)],
-            dst_ref=pbuf.at[pl.ds(slot, leaves)],
-            send_sem=panel_send_sem.at[i],
-            recv_sem=panel_recv_sem.at[26 - i],
+            src_ref=pbuf.at[pl.ds(source, leaves)],
+            dst_ref=pbuf.at[pl.ds(target, leaves)],
+            send_sem=panel_send_sem.at[index],
+            recv_sem=panel_recv_sem.at[index],
             device_id=(dev,),
             device_id_type=MESH,
         )
 
-    x_steps = ((0, 1, 3), (0, 2, 1), (1, 1, 0))
-
-    def send_panel(j, carry):
-        for step, (leaf, leaves, place) in enumerate(x_steps):
-            i = 9 * step + j
-            dev, there, _, oy, oz = panel_partner(i)
-
-            @pl.when(there)
-            def _():
-                slot = ((1 - oz) * 3 + 1 - oy) * 4 + place
-                panel_copy(i, dev, leaf, leaves, slot).start()
-
-        return carry
+    def copy_z(d):
+        return panel_copy(own_slot, 4 * (5 - 2 * d) + 1, 2, d, side_z[d][0])
+
+    def copy_x(d, a):
+        row = 4 * (3 + a)
+        return panel_copy(row + 1 + d, row + 3 - 3 * d, 1, 2 + 3 * d + a, side_x[d][0])
+
+    def copy_y(d, a, n):
+        first, leaves, _ = spans[n]
+        source = 4 * (3 + a) + first
+        target = 4 * (3 * (2 - 2 * d) + a) + first
+        return panel_copy(source, target, leaves, 8 + 9 * d + 3 * a + n, side_y[d][0])
+
+    def panel_jobs():
+        for d in range(2):
+            yield side_z[d][1], copy_z(d)
+        for d in range(2):
+            for a in range(3):
+                yield both(side_x[d][1], layer_ok[a]), copy_x(d, a)
+        for d in range(2):
+            for a in range(3):
+                for n in range(3):
+                    yield both(side_y[d][1], layer_ok[a], spans[n][2]), copy_y(d, a, n)
+
+    def run_if(flag, action):
+        if flag is None:
+            action()
+        else:
+            pl.when(flag)(action)
+
+    def start_x(a):
+        for d in range(2):
+            run_if(both(side_x[d][1], layer_ok[a]), copy_x(d, a).start)
+
+    def start_y(a, n):
+        for d in range(2):
+            run_if(both(side_y[d][1], layer_ok[a], spans[n][2]), copy_y(d, a, n).start)
+
+    for d in range(2):
+        run_if(side_z[d][1], copy_z(d).start)
+    start_x(1)
+    start_y(1, 0)
 
     for r in range(1, 4):
         part_copy(r).wait_recv()
@@ -284,15 +330,7 @@
             device_id_type=MESH,
         )
 
-    def send_cluster(i, carry):
-        @pl.when(cluster_far(4 * i + g))
-        def _():
-            clus_copy(i, parent // 4, 4 * (4 * i + g) + parent % 4).start()
-
-        return carry
-
-    lax.fori_loop(0, 16, send_cluster, 0)
-    lax.fori_loop(0, 9, send_panel, 0)
+    for_each(clusters, lambda i, dev: clus_copy(i, parent // 4, dev).start())
 
     load_raw.wait()
     split_levels(raw, turn, (m0, m1))
@@ -302,17 +340,16 @@
                 first = 49 * dx + 7 * dy + 2
                 table[pl.ds(first, 3)] = jnp.zeros((3, HALF, PAIR), jnp.bfloat16)
 
-    def wait_coef(i, carry):
-        _, there = coef_partner(i)
-
-        @pl.when(there)
-        def _():
-            coef_copy(i, i, me).wait_recv()
-
-        return carry
-
-    lax.fori_loop(0, 27, wait_coef, 0)
-    offsets = [(a, b, c) for a in (-1, 0, 1) for b in (-1, 0, 1) for c in (-1, 0, 1)]
+    for a, d in ((0, 1), (2, 0)):
+        run_if(layer_ok[a], copy_z(d).wait_recv)
+        start_x(a)
+        start_y(a, 0)
+    for a in (1, 0, 2):
+        for n, d in ((1, 1), (2, 0)):
+            run_if(both(spans[n][2], layer_ok[a]), copy_x(d, a).wait_recv)
+            start_y(a, n)
+
+    for_each(coef_partners, lambda i, dev: coef_copy(i, i, me).wait_recv())
     chunks = [list(range(first, min(first + 4, 27))) for first in range(0, 27, 4)]
     for t, chunk in enumerate(chunks):
         rows = x0[pl.ds(chunk[0], len(chunk))].reshape(len(chunk) * RANK, PAIR)
@@ -327,7 +364,7 @@
                 for tx in range(2):
                     column = []
                     for e in chunk:
-                        ex, ey, ez = offsets[e]
+                        ex, ey, ez = OFFSETS[e]
                         for h in range(2):
                             code = (
                                 49 * (2 * ex + h - tx + 3)
@@ -344,20 +381,12 @@
             second = pltpu.roll(acc[:COLS, PAIR:], COLS, 1) + acc[COLS:, PAIR:]
             sum_send[2 * tz + ty, :COLS, :] = jnp.where(lanes < COLS, first, second)
 
-    def wait_cluster(i, carry):
-        @pl.when(cluster_far(4 * i + g))
-        def _():
-            clus_copy(i, i, me).wait_recv()
-
-        return carry
-
-    lax.fori_loop(0, 16, wait_cluster, 0)
+    for_each(clusters, lambda i, dev: clus_copy(i, i, me).wait_recv())
     acc = jnp.zeros((PAIR, PAIR), jnp.float32)
     for t in range(2):
         column = []
         for i in range(8 * t, 8 * t + 8):
-            qx, qy, qz = cluster_position(4 * i + g)
-            column.append(m1[49 * (qx - px + 3) + 7 * (qy - py + 3) + (qz - pz + 3)])
+            column.append(m1[cluster_base + clusters[i][2]])
         rows = x1[pl.ds(8 * t, 8)].reshape(8 * HALF, PAIR)
         acc = acc + jnp.dot(
             rows.T, jnp.concatenate(column, axis=0), preferred_element_type=jnp.float32
@@ -373,33 +402,27 @@
             dst_ref=sum_recv.at[r - 1],
             send_sem=sum_send_sem.at[r - 1],
             recv_sem=sum_recv_sem.at[r - 1],
-            device_id=(4 * parent + (g + r) % 4,),
+            device_id=(mates[r - 1],),
             device_id_type=MESH,
         )
 
     for r in range(1, 4):
         sum_copy(r).start()
 
-    def wait_panel(j, carry):
-        for step, (leaf, leaves, place) in enumerate(x_steps):
-            i = 9 * step + j
-            _, there, _, oy, oz = panel_partner(i)
-
-            @pl.when(there)
-            def _():
-                slot = ((1 - oz) * 3 + 1 - oy) * 4 + place
-                panel_copy(26 - i, me, 0, leaves, slot).wait_recv()
-
-        return carry
-
-    lax.fori_loop(0, 9, wait_panel, 0)
+    for d in range(2):
+        for a in range(3):
+            for n in range(3):
+                run_if(
+                    both(side_y[1 - d][1], layer_ok[a], spans[n][2]), copy_y(d, a, n).wait_recv
+                )
     load_near.wait()
+    load_list.wait()
 
     def slot_of(entry):
         lx = ((entry >> 0) & 1) + 2 * ((entry >> 3) & 1) + 4 * ((entry >> 6) & 1)
         ly = ((entry >> 1) & 1) + 2 * ((entry >> 4) & 1) + 4 * ((entry >> 7) & 1)
         lz = ((entry >> 2) & 1) + 2 * ((entry >> 5) & 1) + 4 * ((entry >> 8) & 1)
-        slot = ((lz - z + 1) * 3 + ly - y + 1) * 4 + lx - 2 * bx + 1
+        slot = ((ly - y + 1) * 3 + lz - z + 1) * 4 + lx - 2 * bx + 1
         return jnp.where(entry < 0, ZERO_SLOT, jnp.clip(slot, 0, ZERO_SLOT))
 
     near_terms = []
@@ -431,39 +454,10 @@
         part_copy(r).wait_send()
         sum_copy(r).wait_send()
 
-    def drain(i, carry):
-        dev, there = coef_partner(i)
-
-        @pl.when(there)
-        def _():
-            coef_copy(i, 26 - i, dev).wait_send()
-
-        return carry
-
-    lax.fori_loop(0, 27, drain, 0)
-
-    def drain_cluster(i, carry):
-        @pl.when(cluster_far(4 * i + g))
-        def _():
-            clus_copy(i, parent // 4, 4 * (4 * i + g) + parent % 4).wait_send()
-
-        return carry
-
-    lax.fori_loop(0, 16, drain_cluster, 0)
-
-    def drain_panel(j, carry):
-        for step, (leaf, leaves, place) in enumerate(x_steps):
-            i = 9 * step + j
-            dev, there, _, oy, oz = panel_partner(i)
-
-            @pl.when(there)
-            def _():
-                slot = ((1 - oz) * 3 + 1 - oy) * 4 + place
-                panel_copy(i, dev, leaf, leaves, slot).wait_send()
-
-        return carry
-
-    lax.fori_loop(0, 9, drain_panel, 0)
+    for_each(coef_partners, lambda i, dev: coef_copy(i, 26 - i, dev).wait_send())
+    for_each(clusters, lambda i, dev: clus_copy(i, parent // 4, dev).wait_send())
+    for flag, copy in panel_jobs():
+        run_if(flag, copy.wait_send)
 
 
 def per_device(panels, basis, transfer, near_blocks, coupling, near_list):
@@ -476,11 +470,12 @@
         kernel,
         name="h2_product",
         out_shape=jax.ShapeDtypeStruct((2, COLS, LEAF), jnp.bfloat16),
-        in_specs=[hbm, hbm, hbm, hbm, hbm, pl.BlockSpec(memory_space=pltpu.SMEM)],
+        in_specs=[hbm] * 6,
         out_specs=vmem,
         scratch_shapes=[
             pltpu.VMEM((37, COLS, LEAF), jnp.bfloat16),
             pltpu.VMEM((2, NNEAR, LEAF, LEAF), jnp.bfloat16),
+            pltpu.SMEM((2, NNEAR), jnp.int32),
             pltpu.VMEM((2, RANK, LEAF), jnp.bfloat16),
             pltpu.VMEM((2, RANK, RANK), jnp.bfloat16),
             pltpu.VMEM((SHIFTS, RANK, PAIR), jnp.bfloat16),
@@ -496,7 +491,7 @@
             pltpu.VMEM((RANK, COLS), jnp.float32),
             pltpu.VMEM((GROUP * RANK, PAIR), jnp.float32),
             pltpu.VMEM((7, PAIR, 2 * PAIR), jnp.bfloat16),
-            dma((5,)),
+            dma((6,)),
             dma((27,)),
             dma((27,)),
             dma((27,)),
@@ -509,9 +504,9 @@
             dma((3,)),
         ],
         compiler_params=pltpu.CompilerParams(
-            collective_id=0, has_side_effects=True, vmem_limit_bytes=56 << 20
+            collective_id=0, has_side_effects=True, vmem_limit_bytes=48 << 20
         ),
-    )(panels, basis, transfer, near_blocks, tables, near_list)
+    )(*[pltpu.with_memory_space_constraint(a, pltpu.HBM) for a in (panels, basis, transfer, near_blocks, tables, near_list)])
 
 
 def solution(mesh):

time: 48.5 us -> 39.6 us (0.82)
  the two profiles are of different devices: /device:TPU:62 before, /device:TPU:21 now
where the time goes in v1:
time: 39.6 us; the launch traced here: 39.5 us
  Pallas kernels  38.8 us (98%)
  local copies, waits for them, and re-layouts  0.63 us (2%)
    pallas_call x1, Pallas kernels, per_device(): pl.pallas_call(kernel, name='h2_product', out_shape=jax.ShapeDtypeStruct(...  38.8 us

profile of v1, /device:TPU:21, one launch (start us, length us, event | category | flops | bytes accessed | tf_op | source)
XLA Modules:
  0.0 39.5 jit_solution(10370116490358863313)
XLA Ops:
  0.0 38.8 %h2_product.1 = bf16[2,64,256]{2,1,0:T(8,128)(2,1)S(1)} custom-call(bf16[2,64,256]{2,1,0:T(8,128)(2,1)} %panels_ref.1, bf16[2,64,256]{2,1,0:T(8,128)(2,1)} %basis_ref.1, bf16[2,64,64]{2,1,0:T(8,128)(2,1)} %transfer_ref.1, bf16[2,27,256,256]{3,2,1,0:T(8,128)(2,1)} %near_ref.1, bf16[343,64,128]{2,1,0:T(8,128)(2,1)} %bitcast.5, s32[2,27]{1,0:T(2,128)} %list_hbm.1), custom_call_target="tpu_custom_call" | custom-call | tf_op jit(solution)/shard_map/h2_product/pallas_call | solution.py:469
  38.9 0.6 %copy.9 = bf16[2,64,256]{2,1,0:T(8,128)(2,1)} copy(bf16[2,64,256]{2,1,0:T(8,128)(2,1)S(1)} %h2_product.1) | data formatting | bytes 131072

commit v2 on v1

--- a/solution.py
+++ b/solution.py
@@ -38,29 +38,6 @@
 
 OFFSETS = [(a, b, c) for a in (-1, 0, 1) for b in (-1, 0, 1) for c in (-1, 0, 1)]
 CENTRE = 13
-
-
-def neighbours(position, sizes, weights):
-    axes = []
-    for here, size, bits in zip(position, sizes, weights):
-        steps = {}
-        for step in (-1, 0, 1):
-            there = here + step
-            share = sum(weight * bit(there, k) for k, weight in enumerate(bits))
-            steps[step] = (share, {-1: here > 0, 0: None, 1: here < size - 1}[step])
-        axes.append(steps)
-    found = []
-    for offset in OFFSETS:
-        parts = [axes[a][offset[a]] for a in range(3)]
-        valid = [ok for _, ok in parts if ok is not None]
-        there = None
-        for ok in valid:
-            there = ok if there is None else there & ok
-        found.append((sum(share for share, _ in parts), there))
-    total = 1
-    for here, size in zip(position, sizes):
-        total = total * (1 + jnp.where(here > 0, 1, 0) + jnp.where(here < size - 1, 1, 0))
-    return found, total - 1
 
 
 def split_rows(scratch, value):
@@ -162,10 +139,16 @@
     side_y = [(place_of((bx, y + d, z)), ok) for d, ok in ((-1, y > 0), (1, y < 7))]
     side_z = [(place_of((bx, y, z + d)), ok) for d, ok in ((-1, z > 0), (1, z < 7))]
     panel_count = ones([ok for _, ok in side_x + side_y + side_z])
-    coef_partners, coef_count = neighbours(
-        (px, py, pz), (4, 4, 4), ((4, 32), (8, 64), (16, 128))
-    )
-    coef_partners = [(dev + g, there) for dev, there in coef_partners]
+    def device_of(tx, ty, tz):
+        share_x = 4 * bit(tx, 0) + 32 * bit(tx, 1)
+        share_y = 8 * bit(ty, 0) + 64 * bit(ty, 1)
+        share_z = 16 * bit(tz, 0) + 128 * bit(tz, 1)
+        return share_x + share_y + share_z + g
+
+    coef_x = [(device_of(px + d, py, pz), ok) for d, ok in ((-1, px > 0), (1, px < 3))]
+    coef_y = [(device_of(px, py + d, pz), ok) for d, ok in ((-1, py > 0), (1, py < 3))]
+    coef_z = [(device_of(px, py, pz + d), ok) for d, ok in ((-1, pz > 0), (1, pz < 3))]
+    coef_count = ones([ok for _, ok in coef_x + coef_y + coef_z])
 
     def close(q, p):
         return (q - p < 2) & (p - q < 2)
@@ -201,7 +184,7 @@
     for dev in mates:
         greet(0, dev)
     for_each(side_x + side_y + side_z, greet)
-    for_each(coef_partners, greet)
+    for_each(coef_x + coef_y + coef_z, greet)
     for_each(clusters, greet)
     count = panel_count + coef_count + cluster_count + 3
 
@@ -240,18 +223,6 @@
     for r in range(1, 4):
         part_copy(r).start()
 
-    def coef_copy(i, slot, dev):
-        return pltpu.make_async_remote_copy(
-            src_ref=x0.at[13],
-            dst_ref=x0.at[slot],
-            send_sem=coef_send_sem.at[i],
-            recv_sem=coef_recv_sem.at[slot],
-            device_id=(dev,),
-            device_id_type=MESH,
-        )
-
-    for_each(coef_partners, lambda i, dev: coef_copy(i, 26 - i, dev).start())
-
     layer_ok = (side_z[0][1], None, side_z[1][1])
     spans = ((1, 2, None), (0, 1, side_x[0][1]), (3, 1, side_x[1][1]))
 
@@ -261,6 +232,12 @@
             if flag is not None:
                 result = flag if result is None else result & flag
         return result
+
+    def run_if(flag, action):
+        if flag is None:
+            action()
+        else:
+            pl.when(flag)(action)
 
     def panel_copy(source, target, leaves, index, dev):
         return pltpu.make_async_remote_copy(
@@ -271,6 +248,38 @@
             device_id=(dev,),
             device_id_type=MESH,
         )
+
+    def coef_copy(source, target, index, dev):
+        return pltpu.make_async_remote_copy(
+            src_ref=x0.at[source],
+            dst_ref=x0.at[target],
+            send_sem=coef_send_sem.at[index],
+            recv_sem=coef_recv_sem.at[index],
+            device_id=(dev,),
+            device_id_type=MESH,
+        )
+
+    coef_layers = (coef_z[0][1], None, coef_z[1][1])
+    coef_sides = ((0, None), (-1, coef_y[0][1]), (1, coef_y[1][1]))
+
+    def coef_to_z(d):
+        return coef_z[d][1], coef_copy(CENTRE, CENTRE + 1 - 2 * d, d, coef_z[d][0])
+
+    def coef_to_y(d, a):
+        flag = both(coef_y[d][1], coef_layers[a])
+        return flag, coef_copy(12 + a, 15 - 6 * d + a, 2 + 3 * d + a, coef_y[d][0])
+
+    def coef_to_x(d, a, n):
+        ey, ok = coef_sides[n]
+        flag = both(coef_x[d][1], coef_layers[a], ok)
+        source = 12 + 3 * ey + a
+        return flag, coef_copy(
+            source, source + 9 - 18 * d, 8 + 9 * d + 3 * a + n, coef_x[d][0]
+        )
+
+    def start(jobs):
+        for flag, copy in jobs:
+            run_if(flag, copy.start)
 
     def copy_z(d):
         return panel_copy(own_slot, 4 * (5 - 2 * d) + 1, 2, d, side_z[d][0])
@@ -296,12 +305,6 @@
                 for n in range(3):
                     yield both(side_y[d][1], layer_ok[a], spans[n][2]), copy_y(d, a, n)
 
-    def run_if(flag, action):
-        if flag is None:
-            action()
-        else:
-            pl.when(flag)(action)
-
     def start_x(a):
         for d in range(2):
             run_if(both(side_x[d][1], layer_ok[a]), copy_x(d, a).start)
@@ -310,9 +313,12 @@
         for d in range(2):
             run_if(both(side_y[d][1], layer_ok[a], spans[n][2]), copy_y(d, a, n).start)
 
+    start([coef_to_z(d) for d in range(2)])
     for d in range(2):
         run_if(side_z[d][1], copy_z(d).start)
+    start([coef_to_y(d, 1) for d in range(2)])
     start_x(1)
+    start([coef_to_x(d, 1, 0) for d in range(2)])
     start_y(1, 0)
 
     for r in range(1, 4):
@@ -341,15 +347,27 @@
                 table[pl.ds(first, 3)] = jnp.zeros((3, HALF, PAIR), jnp.bfloat16)
 
     for a, d in ((0, 1), (2, 0)):
+        run_if(coef_layers[a], coef_to_z(d)[1].wait_recv)
+        start([coef_to_y(e, a) for e in range(2)])
+        start([coef_to_x(e, a, 0) for e in range(2)])
+    for a, d in ((0, 1), (2, 0)):
         run_if(layer_ok[a], copy_z(d).wait_recv)
         start_x(a)
         start_y(a, 0)
     for a in (1, 0, 2):
         for n, d in ((1, 1), (2, 0)):
+            run_if(both(coef_sides[n][1], coef_layers[a]), coef_to_y(d, a)[1].wait_recv)
+            start([coef_to_x(e, a, n) for e in range(2)])
+    for a in (1, 0, 2):
+        for n, d in ((1, 1), (2, 0)):
             run_if(both(spans[n][2], layer_ok[a]), copy_x(d, a).wait_recv)
             start_y(a, n)
 
-    for_each(coef_partners, lambda i, dev: coef_copy(i, i, me).wait_recv())
+    for d in range(2):
+        for a in range(3):
+            for n in range(3):
+                flag = both(coef_x[1 - d][1], coef_layers[a], coef_sides[n][1])
+                run_if(flag, coef_to_x(d, a, n)[1].wait_recv)
     chunks = [list(range(first, min(first + 4, 27))) for first in range(0, 27, 4)]
     for t, chunk in enumerate(chunks):
         rows = x0[pl.ds(chunk[0], len(chunk))].reshape(len(chunk) * RANK, PAIR)
@@ -454,7 +472,11 @@
         part_copy(r).wait_send()
         sum_copy(r).wait_send()
 
-    for_each(coef_partners, lambda i, dev: coef_copy(i, 26 - i, dev).wait_send())
+    coef_jobs = [coef_to_z(d) for d in range(2)]
+    coef_jobs += [coef_to_y(d, a) for d in range(2) for a in range(3)]
+    coef_jobs += [coef_to_x(d, a, n) for d in range(2) for a in range(3) for n in range(3)]
+    for flag, copy in coef_jobs:
+        run_if(flag, copy.wait_send)
     for_each(clusters, lambda i, dev: clus_copy(i, parent // 4, dev).wait_send())
     for flag, copy in panel_jobs():
         run_if(flag, copy.wait_send)

time: 39.6 us -> 34.2 us (0.86)
  the two profiles are of different devices: /device:TPU:21 before, /device:TPU:29 now
where the time goes in v2:
time: 34.2 us
  Pallas kernels  33.5 us (98%)
  local copies, waits for them, and re-layouts  0.63 us (2%)
    pallas_call x1, Pallas kernels, per_device(): pl.pallas_call(kernel, name='h2_product', out_shape=jax.ShapeDtypeStruct(...  33.5 us

profile of v2, /device:TPU:29, one launch (start us, length us, event | category | flops | bytes accessed | tf_op | source)
XLA Modules:
  0.0 34.2 jit_solution(2889934138934490688)
XLA Ops:
  0.0 33.5 %h2_product.1 = bf16[2,64,256]{2,1,0:T(8,128)(2,1)S(1)} custom-call(bf16[2,64,256]{2,1,0:T(8,128)(2,1)} %panels_ref.1, bf16[2,64,256]{2,1,0:T(8,128)(2,1)} %basis_ref.1, bf16[2,64,64]{2,1,0:T(8,128)(2,1)} %transfer_ref.1, bf16[2,27,256,256]{3,2,1,0:T(8,128)(2,1)} %near_ref.1, bf16[343,64,128]{2,1,0:T(8,128)(2,1)} %bitcast.5, s32[2,27]{1,0:T(2,128)} %list_hbm.1), custom_call_target="tpu_custom_call" | custom-call | tf_op jit(solution)/shard_map/h2_product/pallas_call | solution.py:491
  33.5 0.6 %copy.9 = bf16[2,64,256]{2,1,0:T(8,128)(2,1)} copy(bf16[2,64,256]{2,1,0:T(8,128)(2,1)S(1)} %h2_product.1) | data formatting | bytes 131072

commit v3 on v2

--- a/solution.py
+++ b/solution.py
@@ -208,6 +208,18 @@
         )
     cluster_send[...] = split_rows(tmp, part)
 
+    def prepare_tables():
+        load_raw.wait()
+        split_levels(raw, turn, (m0, m1))
+        for table in (m0, m1):
+            for dx in (2, 3, 4):
+                for dy in (2, 3, 4):
+                    first = 49 * dx + 7 * dy + 2
+                    table[pl.ds(first, 3)] = jnp.zeros((3, HALF, PAIR), jnp.bfloat16)
+
+
+    pl.when(z < 4)(prepare_tables)
+
     pl.semaphore_wait(barrier, count)
 
     def part_copy(r):
@@ -338,13 +350,7 @@
 
     for_each(clusters, lambda i, dev: clus_copy(i, parent // 4, dev).start())
 
-    load_raw.wait()
-    split_levels(raw, turn, (m0, m1))
-    for table in (m0, m1):
-        for dx in (2, 3, 4):
-            for dy in (2, 3, 4):
-                first = 49 * dx + 7 * dy + 2
-                table[pl.ds(first, 3)] = jnp.zeros((3, HALF, PAIR), jnp.bfloat16)
+    pl.when(z >= 4)(prepare_tables)
 
     for a, d in ((0, 1), (2, 0)):
         run_if(coef_layers[a], coef_to_z(d)[1].wait_recv)

time: 34.2 us -> 34.2 us (level)
  no operation moved by 1% of the time
where the time goes in v3:
time: 34.2 us
  Pallas kernels  33.5 us (98%)
  local copies, waits for them, and re-layouts  0.63 us (2%)
    pallas_call x1, Pallas kernels, per_device(): pl.pallas_call(kernel, name='h2_product', out_shape=jax.ShapeDtypeStruct(...  33.5 us

profile of v3, /device:TPU:29, one launch (start us, length us, event | category | flops | bytes accessed | tf_op | source)
XLA Modules:
  0.0 34.2 jit_solution(1382614263268432002)
XLA Ops:
  0.0 33.5 %h2_product.1 = bf16[2,64,256]{2,1,0:T(8,128)(2,1)S(1)} custom-call(bf16[2,64,256]{2,1,0:T(8,128)(2,1)} %panels_ref.1, bf16[2,64,256]{2,1,0:T(8,128)(2,1)} %basis_ref.1, bf16[2,64,64]{2,1,0:T(8,128)(2,1)} %transfer_ref.1, bf16[2,27,256,256]{3,2,1,0:T(8,128)(2,1)} %near_ref.1, bf16[343,64,128]{2,1,0:T(8,128)(2,1)} %bitcast.5, s32[2,27]{1,0:T(2,128)} %list_hbm.1), custom_call_target="tpu_custom_call" | custom-call | tf_op jit(solution)/shard_map/h2_product/pallas_call | solution.py:497
  33.5 0.6 %copy.9 = bf16[2,64,256]{2,1,0:T(8,128)(2,1)} copy(bf16[2,64,256]{2,1,0:T(8,128)(2,1)S(1)} %h2_product.1) | data formatting | bytes 131072
